TPU v7x, 128 devices: a whole 4x4x4 slice. The times are simulated.
128 devices in a mesh: stream: 16 (over x, z_hi, core), leaf: 8 (over y, z_lo).
Axes of the slice: x: 4, y: 4, z: 4 (z_hi: 2, z_lo: 2; z = z_hi * 2 + z_lo), core: 2. Of those that a mesh axis runs over, the one named last changes fastest.
Arguments:
- points_rhs: bfloat16 [8192, 32, 128], P(('stream', 'leaf')), may hold values from -6 to 6
- leaf_basis: bfloat16 [8192, 64, 128], P(('stream', 'leaf')), may hold values from -0.5 to 0.5
- transfer: bfloat16 [4096, 64, 128], P(('stream', 'leaf')), may hold values from -0.5 to 0.5
- leaf_coupling: bfloat16 [8192, 64, 256], P(('stream', 'leaf')), may hold values from -0.375 to 0.375
- parent_coupling: bfloat16 [4096, 64, 512], P(('stream', 'leaf')), may hold values from -0.25 to 0.25
- near_blocks: bfloat16 [8192, 3, 128, 128], P(('stream', 'leaf')), may hold values from -0.3125 to 0.3125
- near_offsets: int32 [8192, 3], P(('stream', 'leaf')), may hold values from -2 to 2, as said below
- coupling_offsets: int32 [8192, 4], P(('stream', 'leaf')), may hold values from -5 to 5, as said below
- parent_owner: int32 [4096, 8], P(('stream', 'leaf')), may hold values from 0 to 127, all different within a row; in each aligned block of 32 rows (0 to 31, 32 to 63, ...) at most 4 rows name the same one
- parent_local: int32 [4096, 8], P(('stream', 'leaf')), may hold values from 0 to 31
Outputs:
- product: bfloat16 [8192, 32, 128], P(('stream', 'leaf'))
Inputs may be any that keep to these rules, and one draw needn't show every extreme that they name: `near_offsets`: each row holds 3 different offsets; the first is 0. `coupling_offsets`: each row holds 4 different nonzero offsets, none of which stands in the same row of near_offsets. `parent_owner`: each row names 8 different blocks; the rows of one device name no block more than 4 times, and in every draw some block is named exactly 4 times by the rows of some device.
All inputs are finite; a program needn't handle non-finite values.
Results may differ from a plain program's by a relative error of at most 0.0053.
Values may be sent and summed in bfloat16 or wider, within the bound.
A program may use at most 128 MiB of HBM per device.

v0:
```python
import jax
import jax.numpy as jnp
from jax import lax
from jax.sharding import PartitionSpec as P


def with_halo(value, sides, width):
    edges = {}
    for axis, dim in sides:
        size, length = (lax.axis_size(axis), value.shape[dim])
        up = [(i, (i + 1) % size) for i in range(size - 1)]
        last = lax.slice_in_dim(value, length - width, length, axis=dim)
        first = lax.slice_in_dim(value, 0, width, axis=dim)
        edges[dim] = (
            lax.ppermute(last, axis, up),
            lax.ppermute(first, axis, [(b, a) for a, b in up]),
        )
    done = []
    for _, dim in sides:
        low, high = edges[dim]
        around = [(width, width) if d in done else (0, 0) for d in range(value.ndim)]
        value = jnp.concatenate([jnp.pad(low, around), value, jnp.pad(high, around)], axis=dim)
        done.append(dim)
    return value


def pick_rows(padded, offsets, reach_leaves):
    row_count = offsets.shape[0]
    row_base = jnp.arange(row_count, dtype=jnp.int32)[:, None] + reach_leaves
    return padded[row_base + offsets]


def slot_places(parent_owner, devices, capacity):
    owner_flat = parent_owner.reshape(-1)
    owner_hits = (owner_flat[:, None] == jnp.arange(devices, dtype=jnp.int32)[None, :]).astype(
        jnp.int32
    )
    earlier = jnp.sum((jnp.cumsum(owner_hits, axis=0) - owner_hits) * owner_hits, axis=1)
    return owner_flat * capacity + earlier


def on_device(
    points_rhs,
    leaf_basis,
    transfer,
    leaf_coupling,
    parent_coupling,
    near_blocks,
    near_offsets,
    coupling_offsets,
    parent_owner,
    parent_local,
):
    leaves, rhs_count, leaf_size = points_rhs.shape
    basis_rank = leaf_basis.shape[1]
    parents = transfer.shape[0]
    coupling_slots = coupling_offsets.shape[1]
    parent_slots = parent_owner.shape[1]
    transfer_split = transfer.reshape(parents, basis_rank, 2, basis_rank)
    leaf_coeffs = jnp.einsum(
        "cnp,crp->cnr", points_rhs, leaf_basis, preferred_element_type=jnp.float32
    ).astype(jnp.bfloat16)
    flat_leaf = leaf_coeffs.reshape(leaves, rhs_count * basis_rank)
    padded_points, padded_coeffs = (
        with_halo(points_rhs, ((("stream", "leaf"), 0),), 5),
        with_halo(flat_leaf, ((("stream", "leaf"), 0),), 5),
    )
    point_reach = 5
    child_pairs = leaf_coeffs.reshape(parents, 2, rhs_count, basis_rank)
    parent_coeffs = jnp.einsum(
        "pjnk,prjk->pnr", child_pairs, transfer_split, preferred_element_type=jnp.float32
    ).astype(jnp.bfloat16)
    parent_panel = parent_coupling.reshape(parents, basis_rank, parent_slots, basis_rank)
    devices = lax.axis_size(("stream", "leaf"))
    capacity = max(2, 2 * parent_slots * parents // devices)
    slot_index = slot_places(parent_owner, devices, capacity)
    send_local = (
        jnp.zeros((devices * capacity,), jnp.int32).at[slot_index].set(parent_local.reshape(-1))
    )
    send_local = send_local.reshape(devices, capacity)
    flat_parent = parent_coeffs.reshape(parents, rhs_count * basis_rank)
    found = flat_parent[
        lax.all_to_all(send_local, ("stream", "leaf"), split_axis=0, concat_axis=0, tiled=True)
    ]
    fetched = lax.all_to_all(found, ("stream", "leaf"), split_axis=0, concat_axis=0, tiled=True)
    remote = fetched.reshape(devices * capacity, rhs_count * basis_rank)[slot_index]
    remote = remote.reshape(parents, parent_slots, rhs_count, basis_rank)
    parent_field = jnp.einsum(
        "pknj,prkj->pnr", remote, parent_panel, preferred_element_type=jnp.float32
    )
    sources = pick_rows(padded_coeffs, coupling_offsets, 5).reshape(
        leaves, coupling_slots, rhs_count, basis_rank
    )
    coupling_panel = leaf_coupling.reshape(leaves, basis_rank, coupling_slots, basis_rank)
    leaf_field = jnp.einsum(
        "cknj,crkj->cnr", sources, coupling_panel, preferred_element_type=jnp.float32
    )
    near_rows = pick_rows(padded_points, near_offsets, point_reach)
    near_terms = jnp.einsum(
        "cknj,ckqj->cnq", near_rows, near_blocks, preferred_element_type=jnp.float32
    )
    downward = jnp.einsum(
        "pnr,prjk->pjnk",
        parent_field.astype(jnp.bfloat16),
        transfer_split,
        preferred_element_type=jnp.float32,
    )
    downward = downward.reshape(leaves, rhs_count, basis_rank)
    leaf_total = (leaf_field + downward).astype(jnp.bfloat16)
    far_terms = jnp.einsum(
        "cnr,crp->cnp", leaf_total, leaf_basis, preferred_element_type=jnp.float32
    )
    return (far_terms + near_terms).astype(jnp.bfloat16)


def solution(mesh):
    placed = (
        P(("stream", "leaf"), None, None),
        P(("stream", "leaf"), None, None),
        P(("stream", "leaf"), None, None),
        P(("stream", "leaf"), None, None),
        P(("stream", "leaf"), None, None),
        P(("stream", "leaf"), None, None, None),
        P(("stream", "leaf"), None),
        P(("stream", "leaf"), None),
        P(("stream", "leaf"), None),
        P(("stream", "leaf"), None),
    )
    return jax.shard_map(
        on_device,
        mesh=mesh,
        in_specs=placed,
        out_specs=P(("stream", "leaf"), None, None),
        check_vma=False,
    )
```

profile of v0, /device:TPU:2, one launch (start us, length us, event | category | flops | bytes accessed | tf_op | source)
XLA Modules:
  0.0 103.5 jit_solution(12584649750386224012)
XLA Ops:
  0.0 0.9 copy.27
  1.1 0.7 broadcast_multiply_fusion
  2.3 0.8 copy.31
  3.4 1.4 %scatter_custom_fusion = s32[512]{0:T(512)S(1)} fusion(s32[256]{0:T(256)S(1)} %bitcast.76, s32[256]{0:T(256)S(1)} %reshape.166, s32[]{:T(128)} %constant.7.clone.1), kind=kCustom, calls=%fused_computation.46 | custom fusion | bytes 2052 | tf_op jit(solution)/shard_map/scatter | solution.py:78
  4.8 0.7 all_to_all.11
  5.5 10.5 %all-to-all-start = ((s32[128,1,4]{2,1,0:T(1,128)}), s32[128,1,4]{2,1,0:T(1,128)S(1)}, u32[]{:S(2)}, u32[]{:S(2)}) async-start(s32[128,1,4]{2,1,0:T(1,128)} %bitcast.10), calls=%async_computation | async-start | bytes 131072 | tf_op jit(solution)/shard_map/all_to_all | solution.py:83
  16.1 2.5 %reshape.122 = bf16[32,64,2,64]{3,2,1,0:T(2,128)(2,1)S(1)} reshape(bf16[32,64,128]{2,1,0:T(8,128)(2,1)} %param.12) | data formatting | bytes 1048576 | tf_op jit(solution)/shard_map/reshape | solution.py:59
  18.5 0.6 convolution_convert_fusion
  19.2 0.3 copy-done.1
  19.5 0.5 copy-done.4
  20.0 0.4 fusion.24
  20.4 0.3 reshape.123
  20.7 4.3 %all-to-all-done = s32[128,1,4]{2,1,0:T(1,128)S(1)} async-done(((s32[128,1,4]{2,1,0:T(1,128)}), s32[128,1,4]{2,1,0:T(1,128)S(1)}, u32[]{:S(2)}, u32[]{:S(2)}) %all-to-all-start) | async-done | bytes 2080 | tf_op jit(solution)/shard_map/all_to_all | solution.py:83
  25.2 2.5 %gather_fusion.1 = bf16[512,2048]{1,0:T(8,128)(2,1)S(1)} fusion(bf16[32,2048]{1,0:T(8,128)(2,1)S(1)} %reshape.123, s32[1024]{0:T(1024)S(1)} %pad_clamp_fusion.2), kind=kCustom, calls=%fused_computation.1 | custom fusion | bytes 4196352 | tf_op jit(solution)/shard_map/gather | solution.py:82
  27.6 2.2 %reshape.139 = bf16[128,4,2048]{2,1,0:T(4,128)(2,1)} reshape(bf16[512,2048]{1,0:T(8,128)(2,1)S(1)} %gather_fusion.1) | data formatting | bytes 4194304 | tf_op jit(solution)/shard_map/gather | solution.py:82
  29.9 6.1 %all-to-all-start.1 = ((bf16[128,4,2048]{2,1,0:T(4,128)(2,1)}), bf16[128,4,2048]{2,1,0:T(4,128)(2,1)}, u32[]{:S(2)}, u32[]{:S(2)}) async-start(bf16[128,4,2048]{2,1,0:T(4,128)(2,1)} %reshape.139), calls=%async_computation.1 | async-start | bytes 4194304 | tf_op jit(solution)/shard_map/all_to_all | solution.py:85
  36.1 3.6 %collective-permute-start = (bf16[5,2048]{1,0:T(8,128)(2,1)S(1)}, bf16[5,2048]{1,0:T(8,128)(2,1)S(1)}, u32[]{:S(2)}, u32[]{:S(2)}) collective-permute-start(bf16[5,2048]{1,0:T(8,128)(2,1)S(1)} %slice.25), channel_id=1, source_target_pairs={{0,1},{1,2},{2,3},{3,4},{4,5},{5,6},{6,7},{7,8},{8,9},{9,10},{10,1... | collective-permute-start | bytes 61448 | tf_op jit(solution)/shard_map/ppermute | solution.py:15
  39.8 6.1 %collective-permute-start.1 = (bf16[5,2048]{1,0:T(8,128)(2,1)S(1)}, bf16[5,2048]{1,0:T(8,128)(2,1)S(1)}, u32[]{:S(2)}, u32[]{:S(2)}) collective-permute-start(bf16[5,2048]{1,0:T(8,128)(2,1)S(1)} %slice.27), channel_id=1, source_target_pairs={{1,0},{2,1},{3,2},{4,3},{5,4},{6,5},{7,6},{8,7},{9,8},{10,9},{11,1... | collective-permute-start | bytes 61448 | tf_op jit(solution)/shard_map/ppermute | solution.py:16
  46.0 1.9 %collective-permute-start.2 = (bf16[5,32,128]{2,1,0:T(8,128)(2,1)S(1)}, bf16[5,32,128]{2,1,0:T(8,128)(2,1)S(1)}, u32[]{:S(2)}, u32[]{:S(2)}) collective-permute-start(bf16[5,32,128]{2,1,0:T(8,128)(2,1)S(1)} %get-tuple-element.5), channel_id=1, source_target_pairs={{0,1},{1,2},{2,3},{3,4},{4,5},{5,6},{6,7},{7,8},{8,9},{9,10},{10,1... | collective-permute-start | bytes 122888 | tf_op jit(solution)/shard_map/ppermute | solution.py:15
  48.0 8.0 %collective-permute-start.3 = (bf16[5,32,128]{2,1,0:T(8,128)(2,1)S(1)}, bf16[5,32,128]{2,1,0:T(8,128)(2,1)S(1)}, u32[]{:S(2)}, u32[]{:S(2)}) collective-permute-start(bf16[5,32,128]{2,1,0:T(8,128)(2,1)S(1)} %get-tuple-element.6), channel_id=1, source_target_pairs={{1,0},{2,1},{3,2},{4,3},{5,4},{6,5},{7,6},{8,7},{9,8},{10,9},{11,1... | collective-permute-start | bytes 122888 | tf_op jit(solution)/shard_map/ppermute | solution.py:16
  56.5 0.5 reshape.118
  57.0 6.2 %reshape.128 = bf16[32,64,8,64]{3,2,1,0:T(8,128)(2,1)} reshape(bf16[32,64,512]{2,1,0:T(8,128)(2,1)} %param.14) | data formatting | bytes 4194304 | tf_op jit(solution)/shard_map/reshape | solution.py:73
  63.2 7.1 %reshape.120 = bf16[64,64,4,64]{3,2,1,0:T(4,128)(2,1)} reshape(bf16[64,64,256]{2,1,0:T(8,128)(2,1)} %param.13) | data formatting | bytes 4194304 | tf_op jit(solution)/shard_map/reshape | solution.py:94
  70.4 1.4 %gather_fusion = bf16[256,2048]{1,0:T(8,128)(2,1)S(1)} fusion(bf16[74,2048]{1,0:T(8,128)(2,1)S(1)} %pad_maximum_fusion.1, s32[1024]{0:T(1024)S(1)} %pad_clamp_fusion.3), kind=kCustom, calls=%fused_computation | custom fusion | bytes 2098176 | tf_op jit(solution)/shard_map/gather | solution.py:30
  71.7 3.1 %reshape.119 = bf16[64,4,32,64]{3,2,1,0:T(8,128)(2,1)} reshape(bf16[256,2048]{1,0:T(8,128)(2,1)S(1)} %gather_fusion) | data formatting | bytes 2097152 | tf_op jit(solution)/shard_map/reshape | solution.py:91
  75.0 2.0 %gather_fusion.3 = bf16[192,32,128]{2,1,0:T(8,128)(2,1)} fusion(bf16[74,32,128]{2,1,0:T(8,128)(2,1)S(1)} %pad_maximum_fusion, s32[1024]{0:T(1024)S(1)} %pad_clamp_fusion), kind=kCustom, calls=%fused_computation.3 | custom fusion | bytes 3146496 | tf_op jit(solution)/shard_map/gather | solution.py:30
  77.0 2.5 %reshape.126 = bf16[512,2048]{1,0:T(8,128)(2,1)S(1)} reshape(bf16[128,4,2048]{2,1,0:T(4,128)(2,1)} %all-to-all-done.1) | data formatting | bytes 4194304 | tf_op jit(solution)/shard_map/reshape | solution.py:86
  79.5 2.4 %gather_fusion.2 = bf16[256,2048]{1,0:T(8,128)(2,1)} fusion(bf16[512,2048]{1,0:T(8,128)(2,1)S(1)} %reshape.126, s32[1024]{0:T(1024)S(1)} %pad_clamp_fusion.1), kind=kCustom, calls=%fused_computation.2 | custom fusion | bytes 2098176 | tf_op jit(solution)/shard_map/gather | solution.py:86
  81.9 4.5 %reshape.127 = bf16[32,8,32,64]{3,2,1,0:T(8,128)(2,1)} reshape(bf16[256,2048]{1,0:T(8,128)(2,1)} %gather_fusion.2) | data formatting | bytes 2097152 | tf_op jit(solution)/shard_map/reshape | solution.py:87
  86.4 5.2 %fusion.29 = f32[32,32,2,64]{3,1,2,0:T(8,128)} fusion(bf16[32,8,32,64]{3,2,1,0:T(8,128)(2,1)} %reshape.127, bf16[32,64,8,64]{3,2,1,0:T(8,128)(2,1)} %reshape.128, bf16[32,64,2,64]{3,2,1,0:T(2,128)(2,1)S(1)} %copy-done.2), kind=kOutput, calls=%fused_computation.22 | convolution fusion | flops 83951616 | bytes 4194304 | tf_op jit(solution)/shard_map/pnr,prjk->pjnk/dot_general | solution.py:102
  91.6 5.7 %fusion.16 = f32[64,32,128]{2,1,0:T(8,128)} fusion(bf16[64,64,128]{2,1,0:T(8,128)(2,1)S(1)} %copy-done, f32[64,32,64]{2,1,0:T(8,128)} %bitcast.70, bf16[64,4,32,64]{3,2,1,0:T(8,128)(2,1)} %reshape.119, bf16[64,64,4,64]{3,2,1,0:T(4,128)(2,1)} %reshape.120), kind=kOutput, calls=%fused_computation.16 | convolution fusion | flops 100925440 | bytes 5767168 | tf_op jit(solution)/shard_map/cnr,crp->cnp/dot_general | solution.py:110
  97.3 6.2 %fusion.14 = bf16[64,32,128]{2,1,0:T(8,128)(2,1)} fusion(f32[64,32,128]{2,1,0:T(8,128)} %fusion.16, bf16[64,3,32,128]{3,2,1,0:T(8,128)(2,1)S(1)} %bitcast.68, bf16[64,3,128,128]{3,2,1,0:T(8,128)(2,1)} %param.15), kind=kOutput, calls=%fused_computation.14 | convolution fusion | flops 201850880 | bytes 9437184 | tf_op jit(solution)/shard_map/cknj,ckqj->cnq/dot_general | solution.py:99
  (57 shorter events, 2.0 us)
Async XLA Ops:
  0.0 18.5 %copy-start = (bf16[64,64,128]{2,1,0:T(8,128)(2,1)S(1)}, bf16[64,64,128]{2,1,0:T(8,128)(2,1)}, u32[]{:S(2)}) copy-start(bf16[64,64,128]{2,1,0:T(8,128)(2,1)} %param.11) | copy-start | bytes 3145732
  0.0 18.5 %copy-start.6 = (bf16[64,32,128]{2,1,0:T(8,128)(2,1)S(1)}, bf16[64,32,128]{2,1,0:T(8,128)(2,1)}, u32[]{:S(2)}) copy-start(bf16[64,32,128]{2,1,0:T(8,128)(2,1)} %param.10) | copy-start | bytes 1572868
  5.5 19.5 %all-to-all-start = ((s32[128,1,4]{2,1,0:T(1,128)}), s32[128,1,4]{2,1,0:T(1,128)S(1)}, u32[]{:S(2)}, u32[]{:S(2)}) async-start(s32[128,1,4]{2,1,0:T(1,128)} %bitcast.10), calls=%async_computation | async-start | bytes 131072 | tf_op jit(solution)/shard_map/all_to_all | solution.py:83
  18.5 1.0 copy-start.1
  19.2 0.8 copy-start.4
  29.9 6.1 %copy-start.5 = (bf16[64,32,64]{2,1,0:T(8,128)(2,1)S(1)}, bf16[64,32,64]{2,1,0:T(8,128)(2,1)}, u32[]{:S(2)}) copy-start(bf16[64,32,64]{2,1,0:T(8,128)(2,1)} %copy-done.4) | copy-start | bytes 786436
  29.9 16.1 %copy-start.7 = (bf16[64,32,128]{2,1,0:T(8,128)(2,1)S(1)}, bf16[64,32,128]{2,1,0:T(8,128)(2,1)}, u32[]{:S(2)}) copy-start(bf16[64,32,128]{2,1,0:T(8,128)(2,1)} %param.10) | copy-start | bytes 1572868
  29.9 26.2 %copy-start.8 = (s32[64,4]{0,1:T(4,128)S(1)}, s32[64,4]{0,1:T(4,128)}, u32[]{:S(2)}) copy-start(s32[64,4]{0,1:T(4,128)} %param.17) | copy-start | bytes 3076
  29.9 26.4 %copy-start.9 = (s32[64,3]{0,1:T(4,128)S(1)}, s32[64,3]{0,1:T(4,128)}, u32[]{:S(2)}) copy-start(s32[64,3]{0,1:T(4,128)} %param.16) | copy-start | bytes 2308
  29.9 47.1 %all-to-all-start.1 = ((bf16[128,4,2048]{2,1,0:T(4,128)(2,1)}), bf16[128,4,2048]{2,1,0:T(4,128)(2,1)}, u32[]{:S(2)}, u32[]{:S(2)}) async-start(bf16[128,4,2048]{2,1,0:T(4,128)(2,1)} %reshape.139), calls=%async_computation.1 | async-start | bytes 4194304 | tf_op jit(solution)/shard_map/all_to_all | solution.py:85
  36.1 34.2 %collective-permute-start = (bf16[5,2048]{1,0:T(8,128)(2,1)S(1)}, bf16[5,2048]{1,0:T(8,128)(2,1)S(1)}, u32[]{:S(2)}, u32[]{:S(2)}) collective-permute-start(bf16[5,2048]{1,0:T(8,128)(2,1)S(1)} %slice.25), channel_id=1, source_target_pairs={{0,1},{1,2},{2,3},{3,4},{4,5},{5,6},{6,7},{7,8},{8,9},{9,10},{10,1... | collective-permute-start | bytes 61448 | tf_op jit(solution)/shard_map/ppermute | solution.py:15
  39.8 30.4 %collective-permute-start.1 = (bf16[5,2048]{1,0:T(8,128)(2,1)S(1)}, bf16[5,2048]{1,0:T(8,128)(2,1)S(1)}, u32[]{:S(2)}, u32[]{:S(2)}) collective-permute-start(bf16[5,2048]{1,0:T(8,128)(2,1)S(1)} %slice.27), channel_id=1, source_target_pairs={{1,0},{2,1},{3,2},{4,3},{5,4},{6,5},{7,6},{8,7},{9,8},{10,9},{11,1... | collective-permute-start | bytes 61448 | tf_op jit(solution)/shard_map/ppermute | solution.py:16
  46.0 28.8 %collective-permute-start.2 = (bf16[5,32,128]{2,1,0:T(8,128)(2,1)S(1)}, bf16[5,32,128]{2,1,0:T(8,128)(2,1)S(1)}, u32[]{:S(2)}, u32[]{:S(2)}) collective-permute-start(bf16[5,32,128]{2,1,0:T(8,128)(2,1)S(1)} %get-tuple-element.5), channel_id=1, source_target_pairs={{0,1},{1,2},{2,3},{3,4},{4,5},{5,6},{6,7},{7,8},{8,9},{9,10},{10,1... | collective-permute-start | bytes 122888 | tf_op jit(solution)/shard_map/ppermute | solution.py:15
  48.0 26.9 %collective-permute-start.3 = (bf16[5,32,128]{2,1,0:T(8,128)(2,1)S(1)}, bf16[5,32,128]{2,1,0:T(8,128)(2,1)S(1)}, u32[]{:S(2)}, u32[]{:S(2)}) collective-permute-start(bf16[5,32,128]{2,1,0:T(8,128)(2,1)S(1)} %get-tuple-element.6), channel_id=1, source_target_pairs={{1,0},{2,1},{3,2},{4,3},{5,4},{6,5},{7,6},{8,7},{9,8},{10,9},{11,1... | collective-permute-start | bytes 122888 | tf_op jit(solution)/shard_map/ppermute | solution.py:16
  81.9 4.5 %copy-start.2 = (bf16[32,64,2,64]{3,2,1,0:T(2,128)(2,1)S(1)}, bf16[32,64,2,64]{3,2,1,0:T(2,128)(2,1)}, u32[]{:S(2)}) copy-start(bf16[32,64,2,64]{3,2,1,0:T(2,128)(2,1)} %copy-done.1) | copy-start | bytes 1572868
  91.6 5.7 %copy-start.3 = (bf16[192,32,128]{2,1,0:T(8,128)(2,1)S(1)}, bf16[192,32,128]{2,1,0:T(8,128)(2,1)}, u32[]{:S(2)}) copy-start(bf16[192,32,128]{2,1,0:T(8,128)(2,1)} %gather_fusion.3) | copy-start | bytes 4718596
where the time goes:
time: 104 us; the launch traced here: 103 us
  local copies, waits for them, and re-layouts  43 us (41%)
  starting transfers between devices  36.4 us (35%)
  matrix products  18.1 us (17%)
  waiting for transfers between devices  4.35 us (4%)
  other arithmetic  1.36 us (1%)
    ppermute x2, starting transfers between devices, with_halo(): lax.ppermute(first, axis, [(b, a) for a, b in up])  14.2 us
    all_to_all x1, starting transfers between devices, on_device(): lax.all_to_all(send_local, ('stream', 'leaf'), split_axis=0, concat_axis=...  10.5 us
    reshape x1, local copies, waits for them, and re-layouts, on_device(): leaf_coupling.reshape(leaves, basis_rank, coupling_slots, basis_rank)  7.06 us
    reshape x1, local copies, waits for them, and re-layouts, on_device(): parent_coupling.reshape(parents, basis_rank, parent_slots, basis_rank)  6.21 us
    dot_general x1, matrix products, on_device(): jnp.einsum('cknj,ckqj->cnq', near_rows, near_blocks, preferred_element_ty...  6.16 us
    all_to_all x1, starting transfers between devices, on_device(): lax.all_to_all(found, ('stream', 'leaf'), split_axis=0, concat_axis=0, ti...  6.08 us
    dot_general x1, matrix products, on_device(): jnp.einsum('cnr,crp->cnp', leaf_total, leaf_basis, preferred_element_type...  5.68 us
    ppermute x2, starting transfers between devices, with_halo(): lax.ppermute(last, axis, up)  5.56 us
  transfers between devices with their start and end apart: 6, of which 1 were waited for; matrix products, arithmetic and copies ran while one was open for 24% of the time, Pallas kernels for 0%

commit v1 on v0

v1 whole, which is shorter than its diff:
```python
import random

import jax
import jax.numpy as jnp
from jax import lax
from jax.experimental import pallas as pl
from jax.experimental.pallas import tpu as pltpu
from jax.sharding import PartitionSpec as P

MESH = pl.DeviceIdType.MESH
F32 = jnp.float32
BF16 = jnp.bfloat16
I32 = jnp.int32
NDEV = 128
NL = 64
NP = 32
KP = 8
CAP = 4
LAST = (((1,), (1,)), ((), ()))


def send_order():
    offsets = [
        (dx, dy, dz, dc)
        for dx in range(4)
        for dy in range(4)
        for dz in range(4)
        for dc in range(2)
    ][1:]
    random.Random(1).shuffle(offsets)
    hops = lambda o: sum(min(v, 4 - v) for v in o[:3])
    offsets.sort(key=lambda o: -hops(o))
    return offsets


ORDER = send_order()


def dot_last(a, b):
    return lax.dot_general(a, b, LAST, preferred_element_type=F32)


def dot(a, b):
    return jnp.dot(a, b, preferred_element_type=F32)


def kernel(
    points, basis, transfer, leaf_cpl, parent_cpl, near, near_off, cpl_off, owner, local, out,
    pts, bas, tra, lcp, pcp, nea,
    coef, pair_buf, tiles, near_acc, leaf_acc, staged,
    ask, asked, asked_rows, slots_v, ranks,
    send_buf, recv_buf, out_buf,
    asked_s, slots_s,
    in_sems, loc_sem, out_sem, ask_send, ask_recv, halo_send, halo_recv, data_send, data_recv,
):
    s = lax.axis_index("stream")
    l = lax.axis_index("leaf")
    rem = lambda a, b: lax.rem(a, jnp.int32(b))
    div = lambda a, b: lax.div(a, jnp.int32(b))
    core, zh, x, y, zl = rem(s, 2), rem(div(s, 2), 2), div(s, 4), div(l, 2), rem(l, 2)
    z = zh * 2 + zl
    me = s * 8 + l
    xs = [rem(x + i, 4) * 4 for i in range(4)]
    ys = [rem(y + i, 4) * 2 for i in range(4)]
    zs = [rem(z + i, 4) for i in range(4)]
    zhs = [div(v, 2) * 2 for v in zs]
    zls = [rem(v, 2) for v in zs]
    cs = [core, 1 - core]

    def place(o):
        dx, dy, dz, dc = o
        return xs[dx] + zhs[dz] + cs[dc], ys[dy] + zls[dz]

    following = rem(me + 1, NDEV)
    previous = rem(me + NDEV - 1, NDEV)
    next_dev = (div(following, 8), rem(following, 8))
    prev_dev = (div(previous, 8), rem(previous, 8))

    loads = []
    for n, (src, dst) in enumerate((
        (points, pts.at[pl.ds(2, NL)]), (basis, bas), (transfer, tra),
        (near, nea), (leaf_cpl, lcp), (parent_cpl, pcp),
    )):
        c = pltpu.make_async_copy(src, dst, in_sems.at[n])
        c.start()
        loads.append(c)

    barrier = pltpu.get_barrier_semaphore()
    for o in ORDER:
        pl.semaphore_signal(barrier, inc=1, device_id=place(o), device_id_type=MESH)

    lane = lax.broadcasted_iota(I32, (NP, NDEV), 1)
    own = owner[...]
    loc = local[...]
    hits = jnp.zeros((NP, NDEV), I32)
    wanted = jnp.zeros((NP, NDEV), I32)
    for k in range(KP):
        eq = own[:, k:k + 1] == lane
        hits += jnp.where(eq, 1, 0)
        wanted += jnp.where(eq, loc[:, k:k + 1], 0)
    seen = jnp.zeros((1, NDEV), I32)
    rows = [jnp.zeros((1, NDEV), I32) for _ in range(CAP)]
    for p in range(NP):
        ranks[p:p + 1, :] = seen
        hit = hits[p:p + 1, :]
        for q in range(CAP):
            rows[q] = jnp.where((hit > 0) & (seen == q), wanted[p:p + 1, :], rows[q])
        seen = seen + hit
    table = jnp.concatenate(rows + [jnp.zeros((NDEV - CAP, NDEV), I32)], axis=0)
    ask[...] = table.T.reshape(NDEV, 1, NDEV)
    before = ranks[...]
    slot = jnp.zeros((NP, NDEV), I32)
    for k in range(KP):
        eq = own[:, k:k + 1] == lane
        rank = jnp.sum(jnp.where(eq, before, 0), axis=1, keepdims=True)
        slot = jnp.where(lane == k, own[:, k:k + 1] * CAP + rank, slot)
    slots_v[...] = slot
    slot_copy = pltpu.make_async_copy(slots_v, slots_s, loc_sem)
    slot_copy.start()

    for c in loads[:3]:
        c.wait()
    low32 = lax.broadcasted_iota(I32, (32, 128), 1) < 64
    low16 = lax.broadcasted_iota(I32, (16, 128), 1) < 64

    def up_leaf(i, _):
        for u in range(4):
            p = i * 4 + u
            a = pts[pl.ds(2 + 2 * p, 2)].reshape(64, 128)
            b = bas[pl.ds(2 * p, 2)].reshape(128, 128)
            both = dot_last(a, b)
            pair = jnp.where(low32, both[:32], both[32:])
            swap = pltpu.roll(pair, 64, 1)
            pair_buf[p] = pair.astype(BF16)
            coef[5 + 2 * p] = jnp.where(low32, pair, swap).astype(BF16)
            coef[6 + 2 * p] = jnp.where(low32, swap, pair).astype(BF16)
        return 0

    lax.fori_loop(0, NP // 4, up_leaf, 0)

    def up_parent(i, _):
        for u in range(4):
            p = i * 4 + u
            t = tra[p]
            twice = dot_last(pair_buf[p], jnp.concatenate([t, t], axis=0))
            tiles[p] = jnp.where(low16, twice[:16], twice[16:]).astype(BF16)
        return 0

    lax.fori_loop(0, NP // 4, up_parent, 0)

    pl.semaphore_wait(barrier, NDEV - 1)
    for o in ORDER:
        st, lf = place(o)
        pltpu.make_async_remote_copy(
            src_ref=ask.at[st * 8 + lf], dst_ref=asked.at[me], send_sem=ask_send,
            recv_sem=ask_recv, device_id=(st, lf), device_id_type=MESH,
        ).start()
    asked[me] = ask[me]
    halos = []
    for n, (src, dst, dev) in enumerate((
        (pts.at[pl.ds(64, 2)], pts.at[pl.ds(0, 2)], next_dev),
        (pts.at[pl.ds(2, 2)], pts.at[pl.ds(66, 2)], prev_dev),
        (coef.at[pl.ds(64, 5)], coef.at[pl.ds(0, 5)], next_dev),
        (coef.at[pl.ds(5, 5)], coef.at[pl.ds(69, 5)], prev_dev),
    )):
        h = pltpu.make_async_remote_copy(
            src_ref=src, dst_ref=dst, send_sem=halo_send.at[n], recv_sem=halo_recv.at[n],
            device_id=dev, device_id_type=MESH,
        )
        h.start()
        halos.append(h)

    def wait_rows(ref, count, sem):
        part = ref.at[pl.ds(0, count)]
        pltpu.make_async_copy(part, part, sem).wait()

    wait_rows(asked, NDEV - 1, ask_recv)
    wait_rows(ask, NDEV - 1, ask_send)
    asked_rows[...] = asked[...].reshape(NDEV, NDEV).T[:8]
    c = pltpu.make_async_copy(asked_rows, asked_s, loc_sem)
    slot_copy.wait()
    c.start()
    c.wait()

    for n, o in enumerate(ORDER):
        st, lf = place(o)
        to = st * 8 + lf
        for q in range(CAP):
            send_buf[n, q] = tiles[asked_s[q, to]]
        pltpu.make_async_remote_copy(
            src_ref=send_buf.at[n], dst_ref=recv_buf.at[me], send_sem=data_send,
            recv_sem=data_recv, device_id=(st, lf), device_id_type=MESH,
        ).start()
    for q in range(CAP):
        recv_buf[me, q] = tiles[asked_s[q, me]]

    for h in halos:
        h.wait()

    @pl.when(me == 0)
    def _():
        pts[0:2] = jnp.zeros((2, 32, 128), BF16)
        coef[0:5] = jnp.zeros((5, 32, 128), BF16)

    @pl.when(me == NDEV - 1)
    def _():
        pts[66:68] = jnp.zeros((2, 32, 128), BF16)
        coef[69:74] = jnp.zeros((5, 32, 128), BF16)

    loads[3].wait()

    def near_body(i, _):
        for u in range(4):
            c = i * 4 + u
            acc = None
            for k in range(3):
                term = dot_last(pts[c + 2 + near_off[c, k]], nea[c, k])
                acc = term if acc is None else acc + term
            near_acc[c] = acc
        return 0

    lax.fori_loop(0, NL // 4, near_body, 0)
    loads[4].wait()

    def leaf_body(i, _):
        for u in range(4):
            p = i * 4 + u
            w = lcp[pl.ds(2 * p, 2)].reshape(128, 256)
            sides = []
            for j in range(2):
                c = 2 * p + j
                src = [coef[c + 5 + cpl_off[c, k]] for k in range(4)]
                sides.append(jnp.concatenate(
                    [jnp.where(low32, src[0], src[1]), jnp.where(low32, src[2], src[3])], axis=1
                ))
            both = dot_last(jnp.concatenate(sides, axis=0), w)
            leaf_acc[p] = jnp.where(low32, both[:32], both[32:])
        return 0

    lax.fori_loop(0, NP // 4, leaf_body, 0)
    loads[5].wait()

    wait_rows(recv_buf, NDEV - 1, data_recv)

    def stage(i, _):
        for u in range(4):
            p = i * 4 + u
            for m in range(KP // 2):
                va = recv_buf[div(slots_s[p, 2 * m], CAP), rem(slots_s[p, 2 * m], CAP)]
                vb = recv_buf[div(slots_s[p, 2 * m + 1], CAP), rem(slots_s[p, 2 * m + 1], CAP)]
                staged[p, 0:16, m * 128:(m + 1) * 128] = jnp.where(low16, va, pltpu.roll(vb, 64, 1))
                staged[p, 16:32, m * 128:(m + 1) * 128] = jnp.where(low16, pltpu.roll(va, 64, 1), vb)
        return 0

    lax.fori_loop(0, NP // 4, stage, 0)

    def down(i, _):
        ps = [i * 8 + u for u in range(8)]
        halves = [dot_last(staged[p], pcp[p]).astype(BF16) for p in ps]
        downs = [dot(h, tra[p]) for h, p in zip(halves, ps)]
        for p, d in zip(ps, downs):
            total = leaf_acc[p] + d
            zero = jnp.zeros_like(total)
            both = jnp.concatenate(
                [jnp.where(low32, total, zero), jnp.where(low32, zero, total)], axis=0
            ).astype(BF16)
            far = dot(both, bas[pl.ds(2 * p, 2)].reshape(128, 128))
            res = far + near_acc[pl.ds(2 * p, 2)].reshape(64, 128)
            out_buf[pl.ds(2 * p, 2)] = res.astype(BF16).reshape(2, 32, 128)
        return 0

    lax.fori_loop(0, NP // 8, down, 0)
    o = pltpu.make_async_copy(out_buf, out, out_sem)
    o.start()
    wait_rows(send_buf, NDEV - 1, data_send)
    o.wait()


def on_device(*args):
    anywhere = pl.BlockSpec(memory_space=pl.ANY)
    smem = pl.BlockSpec(memory_space=pltpu.SMEM)
    vmem = pl.BlockSpec(memory_space=pltpu.VMEM)
    dma = pltpu.SemaphoreType.DMA
    return pl.pallas_call(
        kernel,
        out_shape=jax.ShapeDtypeStruct((NL, 32, 128), BF16),
        in_specs=[anywhere] * 6 + [smem] * 2 + [vmem] * 2,
        out_specs=anywhere,
        scratch_shapes=[
            pltpu.VMEM((NL + 4, 32, 128), BF16),
            pltpu.VMEM((NL, 64, 128), BF16),
            pltpu.VMEM((NP, 64, 128), BF16),
            pltpu.VMEM((NL, 64, 256), BF16),
            pltpu.VMEM((NP, 64, 512), BF16),
            pltpu.VMEM((NL, 3, 128, 128), BF16),
            pltpu.VMEM((NL + 10, 32, 128), BF16),
            pltpu.VMEM((NP, 32, 128), BF16),
            pltpu.VMEM((NP, 16, 128), BF16),
            pltpu.VMEM((NL, 32, 128), F32),
            pltpu.VMEM((NP, 32, 128), F32),
            pltpu.VMEM((NP, 32, 512), BF16),
            pltpu.VMEM((NDEV, 1, NDEV), I32),
            pltpu.VMEM((NDEV, 1, NDEV), I32),
            pltpu.VMEM((8, NDEV), I32),
            pltpu.VMEM((NP, NDEV), I32),
            pltpu.VMEM((NP, NDEV), I32),
            pltpu.VMEM((NDEV - 1, CAP, 16, 128), BF16),
            pltpu.VMEM((NDEV, CAP, 16, 128), BF16),
            pltpu.VMEM((NL, 32, 128), BF16),
            pltpu.SMEM((8, NDEV), I32),
            pltpu.SMEM((NP, NDEV), I32),
            dma((6,)), dma, dma, dma, dma, dma((4,)), dma((4,)), dma, dma,
        ],
        compiler_params=pltpu.CompilerParams(
            collective_id=0, has_side_effects=True, vmem_limit_bytes=56 * 1024 * 1024
        ),
        name="h2",
    )(*args)


def solution(mesh):
    both = ("stream", "leaf")
    placed = tuple(P(both, *([None] * n)) for n in (2, 2, 2, 2, 2, 3, 1, 1, 1, 1))
    return jax.shard_map(
        on_device, mesh=mesh, in_specs=placed, out_specs=P(both, None, None), check_vma=False
    )
```

time: 104 us -> 57.7 us (0.55)
  the two profiles are of different devices: /device:TPU:2 before, /device:TPU:1 now
where the time goes in v1:
time: 57.7 us; the launch traced here: 57.2 us
  Pallas kernels  49.9 us (86%)
  local copies, waits for them, and re-layouts  7.35 us (13%)
    pallas_call x1, Pallas kernels, on_device(): pl.pallas_call(kernel, out_shape=jax.ShapeDtypeStruct((NL, 32, 128), BF16...  49.9 us
    unnamed x5, local copies, waits for them, and re-layouts  7.35 us

profile of v1, /device:TPU:1, one launch (start us, length us, event | category | flops | bytes accessed | tf_op | source)
XLA Modules:
  0.0 57.2 jit_solution(14234895123601571615)
XLA Ops:
  0.0 1.4 %copy.13.owner = s32[32,8]{1,0:T(8,128)} copy(s32[32,8]{0,1:T(8,128)} %param.18) | data formatting | bytes 2048 | tf_op args[8]
  1.4 1.4 %copy.14.local = s32[32,8]{1,0:T(8,128)} copy(s32[32,8]{0,1:T(8,128)} %param.19) | data formatting | bytes 2048 | tf_op args[9]
  2.7 1.4 %copy.11.near_off = s32[64,3]{1,0:T(8,128)} copy(s32[64,3]{0,1:T(4,128)} %param.16) | data formatting | bytes 1536 | tf_op args[6]
  4.1 1.4 %copy.12.cpl_off = s32[64,4]{1,0:T(8,128)} copy(s32[64,4]{0,1:T(4,128)} %param.17) | data formatting | bytes 2048 | tf_op args[7]
  5.5 49.9 %h2.1 = bf16[64,32,128]{2,1,0:T(8,128)(2,1)} custom-call(bf16[64,32,128]{2,1,0:T(8,128)(2,1)} %points.1, bf16[64,64,128]{2,1,0:T(8,128)(2,1)} %basis.1, bf16[32,64,128]{2,1,0:T(8,128)(2,1)} %transfer.1, bf16[64,64,256]{2,1,0:T(8,128)(2,1)} %leaf_cpl.1, bf16[32,64,512]{2,1,0:T(8,128)(2,1)} %parent_cpl.1, bf16[64,3,128,128]{3,2,1,0:T(8,128)(2,1)} %near.1, ...), custom_call_target="tpu_custom_call" | custom-call | tf_op jit(solution)/shard_map/h2/pallas_call | solution.py:284
  55.4 1.9 %copy.16 = bf16[64,32,128]{2,1,0:T(8,128)(2,1)} copy(bf16[64,32,128]{2,1,0:T(8,128)(2,1)} %h2.1) | data formatting | bytes 1048576

commit v2 on v1

v2 whole, which is shorter than its diff:
```python
import jax
import jax.numpy as jnp
from jax import lax
from jax.experimental import pallas as pl
from jax.experimental.pallas import tpu as pltpu
from jax.sharding import PartitionSpec as P

MESH = pl.DeviceIdType.MESH
F32 = jnp.float32
BF16 = jnp.bfloat16
I32 = jnp.int32
NDEV = 128
NL = 64
NP = 32
KP = 8
CAP = 4
LAST = (((1,), (1,)), ((), ()))


NQ = 4
ROUTES = ((0, 1, 2), (1, 2, 0), (2, 0, 1), (0, 1, 2))
PARTNERS = [(a, d, dc) for a in range(3) for d in (2, 1, 3) for dc in range(2)] + [(0, 0, 1)]


def dot_last(a, b):
    return lax.dot_general(a, b, LAST, preferred_element_type=F32)


def dot(a, b):
    return jnp.dot(a, b, preferred_element_type=F32)


def kernel(*refs):
    held, recv_buf = refs[-8:-4], refs[-4:]
    body(*refs[:-8], held, recv_buf)


def body(
    points, basis, transfer, leaf_cpl, parent_cpl, near, near_off, cpl_off, owner, local, out,
    pts, bas, tra, lcp, pcp, nea,
    coef, pair_buf, near_acc, leaf_acc, staged,
    turned, ask, asked, slots_v, ranks,
    send_buf, out_buf,
    asked_s, slots_s,
    in_sems, slot_sem, asked_sem, out_sem, ask_send, ask_recv, halo_send, halo_recv,
    held_send, first_recv, second_recv, data_send, data_recv,
    held, recv_buf,
):
    s = lax.axis_index("stream")
    l = lax.axis_index("leaf")
    rem = lambda a, b: lax.rem(a, jnp.int32(b))
    div = lambda a, b: lax.div(a, jnp.int32(b))
    core = rem(s, 2)
    at = (div(s, 4), div(l, 2), rem(div(s, 2), 2) * 2 + rem(l, 2))
    me = s * 8 + l

    adds = (
        lambda v: (v * 4, 0),
        lambda v: (0, v * 2),
        lambda v: (div(v, 2) * 2, rem(v, 2)),
    )
    shifted = [[adds[a](rem(at[a] + d, 4)) for d in range(4)] for a in range(3)]

    def place(a, d, dc):
        st = core if dc == 0 else 1 - core
        lf = 0
        for axis in range(3):
            part = shifted[axis][d if axis == a else 0]
            st = st + part[0]
            lf = lf + part[1]
        return st, lf

    following = rem(me + 1, NDEV)
    previous = rem(me + NDEV - 1, NDEV)
    next_dev = (div(following, 8), rem(following, 8))
    prev_dev = (div(previous, 8), rem(previous, 8))

    loads = []
    for n, (src, dst) in enumerate((
        (points, pts.at[pl.ds(2, NL)]), (basis, bas), (transfer, tra),
        (near, nea), (leaf_cpl, lcp), (parent_cpl, pcp),
    )):
        c = pltpu.make_async_copy(src, dst, in_sems.at[n])
        c.start()
        loads.append(c)

    barrier = pltpu.get_barrier_semaphore()
    for to in [place(*p) for p in PARTNERS] + [next_dev, prev_dev]:
        pl.semaphore_signal(barrier, inc=1, device_id=to, device_id_type=MESH)

    turned[...] = jnp.zeros((NDEV, NDEV), I32)
    turned[0:KP, 0:NP] = owner[...]
    turned[KP:2 * KP, 0:NP] = local[...]
    both_t = turned[...].T
    own = both_t[:NP, 0:KP]
    loc = both_t[:NP, KP:2 * KP]
    lane = lax.broadcasted_iota(I32, (NP, NDEV), 1)
    hits = jnp.zeros((NP, NDEV), I32)
    wanted = jnp.zeros((NP, NDEV), I32)
    for k in range(KP):
        eq = own[:, k:k + 1] == lane
        hits += jnp.where(eq, 1, 0)
        wanted += jnp.where(eq, loc[:, k:k + 1], 0)
    seen = jnp.zeros((1, NDEV), I32)
    rows = [jnp.zeros((1, NDEV), I32) for _ in range(CAP)]
    for p in range(NP):
        ranks[p:p + 1, :] = seen
        hit = hits[p:p + 1, :]
        for q in range(CAP):
            rows[q] = jnp.where((hit > 0) & (seen == q), wanted[p:p + 1, :], rows[q])
        seen = seen + hit
    for q in range(CAP):
        ask[q:q + 1, :] = rows[q]
        asked[len(PARTNERS), q:q + 1, :] = rows[q]

    for c in loads[:3]:
        c.wait()
    low32 = lax.broadcasted_iota(I32, (32, 128), 1) < 64
    low8 = lax.broadcasted_iota(I32, (8, 128), 1) < 64
    low4 = lax.broadcasted_iota(I32, (4, 128), 1) < 64

    def up_leaf(i, _):
        for u in range(8):
            p = i * 8 + u
            a = pts[pl.ds(2 + 2 * p, 2)].reshape(64, 128)
            b = bas[pl.ds(2 * p, 2)].reshape(128, 128)
            both = dot_last(a, b)
            pair = jnp.where(low32, both[:32], both[32:])
            swap = pltpu.roll(pair, 64, 1)
            pair_buf[p] = pair.astype(BF16)
            coef[5 + 2 * p] = jnp.where(low32, pair, swap).astype(BF16)
            coef[6 + 2 * p] = jnp.where(low32, swap, pair).astype(BF16)
        return 0

    lax.fori_loop(0, NP // 8, up_leaf, 0)
    block = [at[r[1]] * 4 + at[r[0]] for r in ROUTES]

    def up_parent(i, _):
        for u in range(8):
            p = i * 8 + u
            t = tra[p]
            twice = dot_last(pair_buf[p], jnp.concatenate([t, t], axis=0))
            for q in range(NQ):
                v = twice[8 * q:8 * q + 8]
                held[q][block[q], p] = jnp.where(low8, v, pltpu.roll(v, 4, 0))[:4].astype(BF16)
        return 0

    lax.fori_loop(0, NP // 8, up_parent, 0)

    pl.semaphore_wait(barrier, len(PARTNERS) + 2)

    def pass_on(q, src, axis, d, sem):
        pltpu.make_async_remote_copy(
            src_ref=held[q].at[src], dst_ref=held[q].at[src], send_sem=held_send.at[q],
            recv_sem=sem.at[q],
            device_id=place(axis, d, 0), device_id_type=MESH,
        ).start()

    for q, r in enumerate(ROUTES):
        for d in (1, 3, 2):
            pass_on(q, block[q], r[0], d, first_recv)
    for n, p in enumerate(PARTNERS):
        back = [i for i, o in enumerate(PARTNERS) if o == (p[0], (4 - p[1]) % 4, p[2])][0]
        pltpu.make_async_remote_copy(
            src_ref=ask, dst_ref=asked.at[back], send_sem=ask_send, recv_sem=ask_recv,
            device_id=place(*p), device_id_type=MESH,
        ).start()
    halos = []
    for n, (src, dst, dev) in enumerate((
        (pts.at[pl.ds(64, 2)], pts.at[pl.ds(0, 2)], next_dev),
        (pts.at[pl.ds(2, 2)], pts.at[pl.ds(66, 2)], prev_dev),
        (coef.at[pl.ds(64, 5)], coef.at[pl.ds(0, 5)], next_dev),
        (coef.at[pl.ds(5, 5)], coef.at[pl.ds(69, 5)], prev_dev),
    )):
        h = pltpu.make_async_remote_copy(
            src_ref=src, dst_ref=dst, send_sem=halo_send.at[n], recv_sem=halo_recv.at[n],
            device_id=dev, device_id_type=MESH,
        )
        h.start()
        halos.append(h)
    for q, r in enumerate(ROUTES):
        for d in (1, 3, 2):
            pass_on(q, block[q], r[1], d, second_recv)

    before = ranks[...]
    coords = (own // 32, rem(own // 2, 4), rem(own // 16, 2) * 2 + rem(own, 2))
    own_core = rem(own // 8, 2)
    slot = jnp.zeros((NP, NDEV), I32)
    for k in range(KP):
        eq = own[:, k:k + 1] == lane
        rank = jnp.sum(jnp.where(eq, before, 0), axis=1, keepdims=True)
        for n, r in enumerate(ROUTES[:3]):
            value = (coords[r[2]] * 2 + own_core) * 64 + (coords[r[1]] * 4 + coords[r[0]]) * 4
            slot = jnp.where(lane == n * KP + k, value[:, k:k + 1] + rank, slot)
    slots_v[...] = slot
    slot_copy = pltpu.make_async_copy(slots_v, slots_s, slot_sem)
    slot_copy.start()

    def wait_part(part, sem):
        pltpu.make_async_copy(part, part, sem).wait()

    for q, r in enumerate(ROUTES):
        wait_part(held[q].at[pl.ds(0, 3)], first_recv.at[q])
        for e in (1, 3, 2):
            src = at[r[1]] * 4 + rem(at[r[0]] + e, 4)
            for d in (1, 3, 2):
                pass_on(q, src, r[1], d, second_recv)

    wait_part(asked.at[pl.ds(0, len(PARTNERS))], ask_recv)
    asked_copy = pltpu.make_async_copy(asked, asked_s, asked_sem)
    asked_copy.start()

    for h in halos:
        h.wait()

    @pl.when(me == 0)
    def _():
        pts[0:2] = jnp.zeros((2, 32, 128), BF16)
        coef[0:5] = jnp.zeros((5, 32, 128), BF16)

    @pl.when(me == NDEV - 1)
    def _():
        pts[66:68] = jnp.zeros((2, 32, 128), BF16)
        coef[69:74] = jnp.zeros((5, 32, 128), BF16)

    loads[3].wait()

    def near_body(i, _):
        for u in range(4):
            c = i * 4 + u
            acc = None
            for k in range(3):
                term = dot_last(pts[c + 2 + near_off[k, c]], nea[c, k])
                acc = term if acc is None else acc + term
            near_acc[c] = acc
        return 0

    lax.fori_loop(0, NL // 4, near_body, 0)
    loads[4].wait()

    def leaf_body(i, _):
        for u in range(4):
            p = i * 4 + u
            w = lcp[pl.ds(2 * p, 2)].reshape(128, 256)
            sides = []
            for j in range(2):
                c = 2 * p + j
                src = [coef[c + 5 + cpl_off[k, c]] for k in range(4)]
                sides.append(jnp.concatenate(
                    [jnp.where(low32, src[0], src[1]), jnp.where(low32, src[2], src[3])], axis=1
                ))
            both = dot_last(jnp.concatenate(sides, axis=0), w)
            leaf_acc[p] = jnp.where(low32, both[:32], both[32:])
        return 0

    lax.fori_loop(0, NP // 4, leaf_body, 0)
    loads[5].wait()
    asked_copy.wait()
    slot_copy.wait()

    base = core * 8
    for q, r in enumerate(ROUTES):
        wait_part(held[q].at[pl.ds(0, 12)], second_recv.at[q])
        fixed = adds[r[2]](at[r[2]])
        fixed = base + fixed[0] * 8 + fixed[1]

        def gather(ref, offset, n):
            def some(i, _):
                add2 = adds[r[1]](i)
                for j in range(4):
                    add1 = adds[r[0]](jnp.int32(j))
                    who = fixed + (add1[0] + add2[0]) * 8 + add1[1] + add2[1]
                    for c in range(CAP):
                        ref[offset + (i * 4 + j) * CAP + c] = held[q][
                            i * 4 + j, asked_s[n, c, who]
                        ]
                return 0

            lax.fori_loop(0, 4, some, 0)

        mine = (at[r[2]] * 2 + core) * 64
        line = [(i, p) for i, p in enumerate(PARTNERS) if p[0] == r[2] and p[1]]
        line.append((len(PARTNERS) - 1, PARTNERS[-1]))
        for m, (n, p) in enumerate(line):
            start = (q * 7 + m) * 64
            gather(send_buf, start, n)
            pltpu.make_async_remote_copy(
                src_ref=send_buf.at[pl.ds(start, 64)], dst_ref=recv_buf[q].at[pl.ds(mine, 64)],
                send_sem=data_send, recv_sem=data_recv.at[q],
                device_id=place(r[2], p[1], p[2]), device_id_type=MESH,
            ).start()
        gather(recv_buf[q], mine, len(PARTNERS))

    for q in range(NQ):
        wait_part(recv_buf[q].at[pl.ds(0, 448)], data_recv.at[q])

        def stage(i, _):
            for u in range(4):
                p = i * 4 + u
                for m in range(KP // 2):
                    k = (q % 3) * KP + 2 * m
                    va = recv_buf[q][slots_s[p, k]]
                    vb = recv_buf[q][slots_s[p, k + 1]]
                    cols = slice(m * 128, (m + 1) * 128)
                    staged[p, 8 * q:8 * q + 4, cols] = jnp.where(low4, va, pltpu.roll(vb, 64, 1))
                    staged[p, 8 * q + 4:8 * q + 8, cols] = jnp.where(low4, pltpu.roll(va, 64, 1), vb)
            return 0

        lax.fori_loop(0, NP // 4, stage, 0)

    def down(i, _):
        ps = [i * 8 + u for u in range(8)]
        halves = [dot_last(staged[p], pcp[p]).astype(BF16) for p in ps]
        downs = [dot(h, tra[p]) for h, p in zip(halves, ps)]
        for p, d in zip(ps, downs):
            total = leaf_acc[p] + d
            zero = jnp.zeros_like(total)
            both = jnp.concatenate(
                [jnp.where(low32, total, zero), jnp.where(low32, zero, total)], axis=0
            ).astype(BF16)
            far = dot(both, bas[pl.ds(2 * p, 2)].reshape(128, 128))
            res = far + near_acc[pl.ds(2 * p, 2)].reshape(64, 128)
            out_buf[pl.ds(2 * p, 2)] = res.astype(BF16).reshape(2, 32, 128)
        return 0

    lax.fori_loop(0, NP // 8, down, 0)
    o = pltpu.make_async_copy(out_buf, out, out_sem)
    o.start()
    wait_part(send_buf, data_send)
    for q in range(NQ):
        wait_part(held[q].at[pl.ds(0, 15)], held_send.at[q])
    wait_part(asked.at[pl.ds(0, len(PARTNERS))], ask_send)
    o.wait()


def on_device(*args):
    anywhere = pl.BlockSpec(memory_space=pl.ANY)
    smem = pl.BlockSpec(memory_space=pltpu.SMEM)
    vmem = pl.BlockSpec(memory_space=pltpu.VMEM)
    dma = pltpu.SemaphoreType.DMA
    return pl.pallas_call(
        kernel,
        out_shape=jax.ShapeDtypeStruct((NL, 32, 128), BF16),
        in_specs=[anywhere] * 6 + [smem] * 2 + [vmem] * 2,
        out_specs=anywhere,
        scratch_shapes=[
            pltpu.VMEM((NL + 4, 32, 128), BF16),
            pltpu.VMEM((NL, 64, 128), BF16),
            pltpu.VMEM((NP, 64, 128), BF16),
            pltpu.VMEM((NL, 64, 256), BF16),
            pltpu.VMEM((NP, 64, 512), BF16),
            pltpu.VMEM((NL, 3, 128, 128), BF16),
            pltpu.VMEM((NL + 10, 32, 128), BF16),
            pltpu.VMEM((NP, 32, 128), BF16),
            pltpu.VMEM((NL, 32, 128), F32),
            pltpu.VMEM((NP, 32, 128), F32),
            pltpu.VMEM((NP, 32, 512), BF16),
            pltpu.VMEM((NDEV, NDEV), I32),
            pltpu.VMEM((CAP, NDEV), I32),
            pltpu.VMEM((len(PARTNERS) + 1, CAP, NDEV), I32),
            pltpu.VMEM((NP, NDEV), I32),
            pltpu.VMEM((NP, NDEV), I32),
            pltpu.VMEM((NQ * 7 * 64, 4, 128), BF16),
            pltpu.VMEM((NL, 32, 128), BF16),
            pltpu.SMEM((len(PARTNERS) + 1, CAP, NDEV), I32),
            pltpu.SMEM((NP, NDEV), I32),
            dma((6,)), dma, dma, dma, dma, dma, dma((4,)), dma((4,)),
            dma((NQ,)), dma((NQ,)), dma((NQ,)), dma, dma((NQ,)),
            *[pltpu.VMEM((16, NP, 4, 128), BF16)] * NQ,
            *[pltpu.VMEM((512, 4, 128), BF16)] * NQ,
        ],
        compiler_params=pltpu.CompilerParams(
            collective_id=0, has_side_effects=True, vmem_limit_bytes=56 * 1024 * 1024
        ),
        name="h2",
    )(*args[:6], *[v.T for v in args[6:]])


def solution(mesh):
    both = ("stream", "leaf")
    placed = tuple(P(both, *([None] * n)) for n in (2, 2, 2, 2, 2, 3, 1, 1, 1, 1))
    return jax.shard_map(
        on_device, mesh=mesh, in_specs=placed, out_specs=P(both, None, None), check_vma=False
    )
```

time: 57.7 us -> 42.3 us (0.73)
  Pallas kernels: 49.9 us -> 40.2 us
  local copies, waits for them, and re-layouts: 7.35 us -> 1.87 us
    pallas_call x1, Pallas kernels: 49.9 us -> 40.2 us  [on_device(): pl.pallas_call(kernel, out_shape=jax.ShapeDtypeStruct((NL, 32, 128), BF16...]
    unnamed x5 -> x1, local copies, waits for them, and re-layouts: 7.35 us -> 1.87 us
where the time goes in v2:
time: 42.3 us; the launch traced here: 42.1 us
  Pallas kernels  40.2 us (95%)
  local copies, waits for them, and re-layouts  1.87 us (4%)
    pallas_call x1, Pallas kernels, on_device(): pl.pallas_call(kernel, out_shape=jax.ShapeDtypeStruct((NL, 32, 128), BF16...  40.2 us
    unnamed x1, local copies, waits for them, and re-layouts  1.87 us

profile of v2, /device:TPU:1, one launch (start us, length us, event | category | flops | bytes accessed | tf_op | source)
XLA Modules:
  0.0 42.1 jit_solution(5349823466282557737)
XLA Ops:
  0.0 40.2 %h2.1 = bf16[64,32,128]{2,1,0:T(8,128)(2,1)} custom-call(bf16[64,32,128]{2,1,0:T(8,128)(2,1)} %refs_0_.1, bf16[64,64,128]{2,1,0:T(8,128)(2,1)} %refs_1_.1, bf16[32,64,128]{2,1,0:T(8,128)(2,1)} %refs_2_.1, bf16[64,64,256]{2,1,0:T(8,128)(2,1)} %refs_3_.1, bf16[32,64,512]{2,1,0:T(8,128)(2,1)} %refs_4_.1, bf16[64,3,128,128]{3,2,1,0:T(8,128)(2,1)} %refs_5_.1, ...), custom_call_target="tpu_custom_call" | custom-call | tf_op jit(solution)/shard_map/h2/pallas_call | solution.py:341
  40.3 1.9 %copy.12 = bf16[64,32,128]{2,1,0:T(8,128)(2,1)} copy(bf16[64,32,128]{2,1,0:T(8,128)(2,1)} %h2.1) | data formatting | bytes 1048576

commit v3 on v2

--- a/solution.py
+++ b/solution.py
@@ -189,7 +189,7 @@
     for k in range(KP):
         eq = own[:, k:k + 1] == lane
         rank = jnp.sum(jnp.where(eq, before, 0), axis=1, keepdims=True)
-        for n, r in enumerate(ROUTES[:3]):
+        for n, r in enumerate(ROUTES):
             value = (coords[r[2]] * 2 + own_core) * 64 + (coords[r[1]] * 4 + coords[r[0]]) * 4
             slot = jnp.where(lane == n * KP + k, value[:, k:k + 1] + rank, slot)
     slots_v[...] = slot
@@ -209,6 +209,43 @@
     wait_part(asked.at[pl.ds(0, len(PARTNERS))], ask_recv)
     asked_copy = pltpu.make_async_copy(asked, asked_s, asked_sem)
     asked_copy.start()
+
+    loads[5].wait()
+    asked_copy.wait()
+    slot_copy.wait()
+
+    base = core * 8
+    for q, r in enumerate(ROUTES):
+        wait_part(held[q].at[pl.ds(0, 12)], second_recv.at[q])
+        fixed = adds[r[2]](at[r[2]])
+        fixed = base + fixed[0] * 8 + fixed[1]
+
+        def gather(ref, offset, n):
+            def some(i, _):
+                add2 = adds[r[1]](i)
+                for j in range(4):
+                    add1 = adds[r[0]](jnp.int32(j))
+                    who = fixed + (add1[0] + add2[0]) * 8 + add1[1] + add2[1]
+                    for c in range(CAP):
+                        ref[offset + (i * 4 + j) * CAP + c] = held[q][
+                            i * 4 + j, asked_s[n, c, who]
+                        ]
+                return 0
+
+            lax.fori_loop(0, 4, some, 0)
+
+        mine = (at[r[2]] * 2 + core) * 64
+        line = [(i, p) for i, p in enumerate(PARTNERS) if p[0] == r[2] and p[1]]
+        line.append((len(PARTNERS) - 1, PARTNERS[-1]))
+        for m, (n, p) in enumerate(line):
+            start = (q * 7 + m) * 64
+            gather(send_buf, start, n)
+            pltpu.make_async_remote_copy(
+                src_ref=send_buf.at[pl.ds(start, 64)], dst_ref=recv_buf[q].at[pl.ds(mine, 64)],
+                send_sem=data_send, recv_sem=data_recv.at[q],
+                device_id=place(r[2], p[1], p[2]), device_id_type=MESH,
+            ).start()
+        gather(recv_buf[q], mine, len(PARTNERS))
 
     for h in halos:
         h.wait()
@@ -254,51 +291,14 @@
         return 0
 
     lax.fori_loop(0, NP // 4, leaf_body, 0)
-    loads[5].wait()
-    asked_copy.wait()
-    slot_copy.wait()
-
-    base = core * 8
-    for q, r in enumerate(ROUTES):
-        wait_part(held[q].at[pl.ds(0, 12)], second_recv.at[q])
-        fixed = adds[r[2]](at[r[2]])
-        fixed = base + fixed[0] * 8 + fixed[1]
-
-        def gather(ref, offset, n):
-            def some(i, _):
-                add2 = adds[r[1]](i)
-                for j in range(4):
-                    add1 = adds[r[0]](jnp.int32(j))
-                    who = fixed + (add1[0] + add2[0]) * 8 + add1[1] + add2[1]
-                    for c in range(CAP):
-                        ref[offset + (i * 4 + j) * CAP + c] = held[q][
-                            i * 4 + j, asked_s[n, c, who]
-                        ]
-                return 0
-
-            lax.fori_loop(0, 4, some, 0)
-
-        mine = (at[r[2]] * 2 + core) * 64
-        line = [(i, p) for i, p in enumerate(PARTNERS) if p[0] == r[2] and p[1]]
-        line.append((len(PARTNERS) - 1, PARTNERS[-1]))
-        for m, (n, p) in enumerate(line):
-            start = (q * 7 + m) * 64
-            gather(send_buf, start, n)
-            pltpu.make_async_remote_copy(
-                src_ref=send_buf.at[pl.ds(start, 64)], dst_ref=recv_buf[q].at[pl.ds(mine, 64)],
-                send_sem=data_send, recv_sem=data_recv.at[q],
-                device_id=place(r[2], p[1], p[2]), device_id_type=MESH,
-            ).start()
-        gather(recv_buf[q], mine, len(PARTNERS))
-
     for q in range(NQ):
         wait_part(recv_buf[q].at[pl.ds(0, 448)], data_recv.at[q])
 
         def stage(i, _):
-            for u in range(4):
-                p = i * 4 + u
+            for u in range(8):
+                p = i * 8 + u
                 for m in range(KP // 2):
-                    k = (q % 3) * KP + 2 * m
+                    k = q * KP + 2 * m
                     va = recv_buf[q][slots_s[p, k]]
                     vb = recv_buf[q][slots_s[p, k + 1]]
                     cols = slice(m * 128, (m + 1) * 128)
@@ -306,10 +306,10 @@
                     staged[p, 8 * q + 4:8 * q + 8, cols] = jnp.where(low4, pltpu.roll(va, 64, 1), vb)
             return 0
 
-        lax.fori_loop(0, NP // 4, stage, 0)
+        lax.fori_loop(0, NP // 8, stage, 0)
 
     def down(i, _):
-        ps = [i * 8 + u for u in range(8)]
+        ps = [i * 16 + u for u in range(16)]
         halves = [dot_last(staged[p], pcp[p]).astype(BF16) for p in ps]
         downs = [dot(h, tra[p]) for h, p in zip(halves, ps)]
         for p, d in zip(ps, downs):
@@ -320,17 +320,14 @@
             ).astype(BF16)
             far = dot(both, bas[pl.ds(2 * p, 2)].reshape(128, 128))
             res = far + near_acc[pl.ds(2 * p, 2)].reshape(64, 128)
-            out_buf[pl.ds(2 * p, 2)] = res.astype(BF16).reshape(2, 32, 128)
-        return 0
-
-    lax.fori_loop(0, NP // 8, down, 0)
-    o = pltpu.make_async_copy(out_buf, out, out_sem)
-    o.start()
+            out[pl.ds(2 * p, 2)] = res.astype(BF16).reshape(2, 32, 128)
+        return 0
+
+    lax.fori_loop(0, NP // 16, down, 0)
     wait_part(send_buf, data_send)
     for q in range(NQ):
         wait_part(held[q].at[pl.ds(0, 15)], held_send.at[q])
     wait_part(asked.at[pl.ds(0, len(PARTNERS))], ask_send)
-    o.wait()
 
 
 def on_device(*args):
@@ -341,8 +338,8 @@
     return pl.pallas_call(
         kernel,
         out_shape=jax.ShapeDtypeStruct((NL, 32, 128), BF16),
-        in_specs=[anywhere] * 6 + [smem] * 2 + [vmem] * 2,
-        out_specs=anywhere,
+        in_specs=[anywhere]*6 + [smem] * 2 + [vmem] * 2,
+        out_specs=vmem,
         scratch_shapes=[
             pltpu.VMEM((NL + 4, 32, 128), BF16),
             pltpu.VMEM((NL, 64, 128), BF16),
@@ -370,10 +367,10 @@
             *[pltpu.VMEM((512, 4, 128), BF16)] * NQ,
         ],
         compiler_params=pltpu.CompilerParams(
-            collective_id=0, has_side_effects=True, vmem_limit_bytes=56 * 1024 * 1024
+            collective_id=0, has_side_effects=True, vmem_limit_bytes=48 * 1024 * 1024
         ),
         name="h2",
-    )(*args[:6], *[v.T for v in args[6:]])
+    )(*[pltpu.with_memory_space_constraint(a, pltpu.HBM) for a in args[:6] + tuple(v.T for v in args[6:])])
 
 
 def solution(mesh):

time: 42.3 us -> 37.3 us (0.88)
  the two profiles are of different devices: /device:TPU:1 before, /device:TPU:96 now
where the time goes in v3:
time: 37.3 us; the launch traced here: 37.1 us
  Pallas kernels  36.3 us (97%)
  local copies, waits for them, and re-layouts  0.8 us (2%)
    pallas_call x1, Pallas kernels, on_device(): pl.pallas_call(kernel, out_shape=jax.ShapeDtypeStruct((NL, 32, 128), BF16...  36.3 us
    unnamed x1, local copies, waits for them, and re-layouts  0.8 us

profile of v3, /device:TPU:96, one launch (start us, length us, event | category | flops | bytes accessed | tf_op | source)
XLA Modules:
  0.0 37.1 jit_solution(11599820598972234463)
XLA Ops:
  0.0 36.3 %h2.1 = bf16[64,32,128]{2,1,0:T(8,128)(2,1)S(1)} custom-call(bf16[64,32,128]{2,1,0:T(8,128)(2,1)} %refs_0_.1, bf16[64,64,128]{2,1,0:T(8,128)(2,1)} %refs_1_.1, bf16[32,64,128]{2,1,0:T(8,128)(2,1)} %refs_2_.1, bf16[64,64,256]{2,1,0:T(8,128)(2,1)} %refs_3_.1, bf16[32,64,512]{2,1,0:T(8,128)(2,1)} %refs_4_.1, bf16[64,3,128,128]{3,2,1,0:T(8,128)(2,1)} %refs_5_.1, ...), custom_call_target="tpu_custom_call" | custom-call | tf_op jit(solution)/shard_map/h2/pallas_call | solution.py:338
  36.3 0.8 %copy.12 = bf16[64,32,128]{2,1,0:T(8,128)(2,1)} copy(bf16[64,32,128]{2,1,0:T(8,128)(2,1)S(1)} %h2.1) | data formatting | bytes 1048576

commit v4 on v3

--- a/solution.py
+++ b/solution.py
@@ -81,12 +81,13 @@
         (near, nea), (leaf_cpl, lcp), (parent_cpl, pcp),
     )):
         c = pltpu.make_async_copy(src, dst, in_sems.at[n])
+        loads.append(c)
+    for c in loads[:3]:
         c.start()
-        loads.append(c)
 
     barrier = pltpu.get_barrier_semaphore()
-    for to in [place(*p) for p in PARTNERS] + [next_dev, prev_dev]:
-        pl.semaphore_signal(barrier, inc=1, device_id=to, device_id_type=MESH)
+    for p in PARTNERS:
+        pl.semaphore_signal(barrier, inc=1, device_id=place(*p), device_id_type=MESH)
 
     turned[...] = jnp.zeros((NDEV, NDEV), I32)
     turned[0:KP, 0:NP] = owner[...]
@@ -115,6 +116,8 @@
 
     for c in loads[:3]:
         c.wait()
+    for c in loads[3:]:
+        c.start()
     low32 = lax.broadcasted_iota(I32, (32, 128), 1) < 64
     low8 = lax.broadcasted_iota(I32, (8, 128), 1) < 64
     low4 = lax.broadcasted_iota(I32, (4, 128), 1) < 64
@@ -147,7 +150,7 @@
 
     lax.fori_loop(0, NP // 8, up_parent, 0)
 
-    pl.semaphore_wait(barrier, len(PARTNERS) + 2)
+    pl.semaphore_wait(barrier, len(PARTNERS))
 
     def pass_on(q, src, axis, d, sem):
         pltpu.make_async_remote_copy(
@@ -165,19 +168,6 @@
             src_ref=ask, dst_ref=asked.at[back], send_sem=ask_send, recv_sem=ask_recv,
             device_id=place(*p), device_id_type=MESH,
         ).start()
-    halos = []
-    for n, (src, dst, dev) in enumerate((
-        (pts.at[pl.ds(64, 2)], pts.at[pl.ds(0, 2)], next_dev),
-        (pts.at[pl.ds(2, 2)], pts.at[pl.ds(66, 2)], prev_dev),
-        (coef.at[pl.ds(64, 5)], coef.at[pl.ds(0, 5)], next_dev),
-        (coef.at[pl.ds(5, 5)], coef.at[pl.ds(69, 5)], prev_dev),
-    )):
-        h = pltpu.make_async_remote_copy(
-            src_ref=src, dst_ref=dst, send_sem=halo_send.at[n], recv_sem=halo_recv.at[n],
-            device_id=dev, device_id_type=MESH,
-        )
-        h.start()
-        halos.append(h)
     for q, r in enumerate(ROUTES):
         for d in (1, 3, 2):
             pass_on(q, block[q], r[1], d, second_recv)
@@ -215,8 +205,22 @@
     slot_copy.wait()
 
     base = core * 8
+    halos = []
     for q, r in enumerate(ROUTES):
         wait_part(held[q].at[pl.ds(0, 12)], second_recv.at[q])
+        if q == 0:
+            for n, (src, dst, dev) in enumerate((
+                (pts.at[pl.ds(64, 2)], pts.at[pl.ds(0, 2)], next_dev),
+                (pts.at[pl.ds(2, 2)], pts.at[pl.ds(66, 2)], prev_dev),
+                (coef.at[pl.ds(64, 5)], coef.at[pl.ds(0, 5)], next_dev),
+                (coef.at[pl.ds(5, 5)], coef.at[pl.ds(69, 5)], prev_dev),
+            )):
+                h = pltpu.make_async_remote_copy(
+                    src_ref=src, dst_ref=dst, send_sem=halo_send.at[n], recv_sem=halo_recv.at[n],
+                    device_id=dev, device_id_type=MESH,
+                )
+                h.start()
+                halos.append(h)
         fixed = adds[r[2]](at[r[2]])
         fixed = base + fixed[0] * 8 + fixed[1]
 

time: 37.3 us -> 39.8 us (1.067)
  the two profiles are of different devices: /device:TPU:96 before, /device:TPU:1 now
where the time goes in v4:
time: 39.8 us; the launch traced here: 39.6 us
  Pallas kernels  38.8 us (97%)
  local copies, waits for them, and re-layouts  0.8 us (2%)
    pallas_call x1, Pallas kernels, on_device(): pl.pallas_call(kernel, out_shape=jax.ShapeDtypeStruct((NL, 32, 128), BF16...  38.8 us

profile of v4, /device:TPU:1, one launch (start us, length us, event | category | flops | bytes accessed | tf_op | source)
XLA Modules:
  0.0 39.6 jit_solution(6585617389906926330)
XLA Ops:
  0.0 38.8 %h2.1 = bf16[64,32,128]{2,1,0:T(8,128)(2,1)S(1)} custom-call(bf16[64,32,128]{2,1,0:T(8,128)(2,1)} %refs_0_.1, bf16[64,64,128]{2,1,0:T(8,128)(2,1)} %refs_1_.1, bf16[32,64,128]{2,1,0:T(8,128)(2,1)} %refs_2_.1, bf16[64,64,256]{2,1,0:T(8,128)(2,1)} %refs_3_.1, bf16[32,64,512]{2,1,0:T(8,128)(2,1)} %refs_4_.1, bf16[64,3,128,128]{3,2,1,0:T(8,128)(2,1)} %refs_5_.1, ...), custom_call_target="tpu_custom_call" | custom-call | tf_op jit(solution)/shard_map/h2/pallas_call | solution.py:342
  38.8 0.8 %copy.12 = bf16[64,32,128]{2,1,0:T(8,128)(2,1)} copy(bf16[64,32,128]{2,1,0:T(8,128)(2,1)S(1)} %h2.1) | data formatting | bytes 1048576

commit v5 on v2

--- a/solution.py
+++ b/solution.py
@@ -189,7 +189,7 @@
     for k in range(KP):
         eq = own[:, k:k + 1] == lane
         rank = jnp.sum(jnp.where(eq, before, 0), axis=1, keepdims=True)
-        for n, r in enumerate(ROUTES[:3]):
+        for n, r in enumerate(ROUTES):
             value = (coords[r[2]] * 2 + own_core) * 64 + (coords[r[1]] * 4 + coords[r[0]]) * 4
             slot = jnp.where(lane == n * KP + k, value[:, k:k + 1] + rank, slot)
     slots_v[...] = slot
@@ -223,24 +223,11 @@
         pts[66:68] = jnp.zeros((2, 32, 128), BF16)
         coef[69:74] = jnp.zeros((5, 32, 128), BF16)
 
-    loads[3].wait()
-
-    def near_body(i, _):
-        for u in range(4):
-            c = i * 4 + u
-            acc = None
-            for k in range(3):
-                term = dot_last(pts[c + 2 + near_off[k, c]], nea[c, k])
-                acc = term if acc is None else acc + term
-            near_acc[c] = acc
-        return 0
-
-    lax.fori_loop(0, NL // 4, near_body, 0)
     loads[4].wait()
 
     def leaf_body(i, _):
-        for u in range(4):
-            p = i * 4 + u
+        for u in range(8):
+            p = i * 8 + u
             w = lcp[pl.ds(2 * p, 2)].reshape(128, 256)
             sides = []
             for j in range(2):
@@ -253,7 +240,7 @@
             leaf_acc[p] = jnp.where(low32, both[:32], both[32:])
         return 0
 
-    lax.fori_loop(0, NP // 4, leaf_body, 0)
+    lax.fori_loop(0, NP // 8, leaf_body, 0)
     loads[5].wait()
     asked_copy.wait()
     slot_copy.wait()
@@ -291,14 +278,27 @@
             ).start()
         gather(recv_buf[q], mine, len(PARTNERS))
 
+    loads[3].wait()
+
+    def near_body(i, _):
+        for u in range(8):
+            c = i * 8 + u
+            acc = None
+            for k in range(3):
+                term = dot_last(pts[c + 2 + near_off[k, c]], nea[c, k])
+                acc = term if acc is None else acc + term
+            near_acc[c] = acc
+        return 0
+
+    lax.fori_loop(0, NL // 8, near_body, 0)
     for q in range(NQ):
         wait_part(recv_buf[q].at[pl.ds(0, 448)], data_recv.at[q])
 
         def stage(i, _):
-            for u in range(4):
-                p = i * 4 + u
+            for u in range(8):
+                p = i * 8 + u
                 for m in range(KP // 2):
-                    k = (q % 3) * KP + 2 * m
+                    k = q * KP + 2 * m
                     va = recv_buf[q][slots_s[p, k]]
                     vb = recv_buf[q][slots_s[p, k + 1]]
                     cols = slice(m * 128, (m + 1) * 128)
@@ -306,10 +306,10 @@
                     staged[p, 8 * q + 4:8 * q + 8, cols] = jnp.where(low4, pltpu.roll(va, 64, 1), vb)
             return 0
 
-        lax.fori_loop(0, NP // 4, stage, 0)
+        lax.fori_loop(0, NP // 8, stage, 0)
 
     def down(i, _):
-        ps = [i * 8 + u for u in range(8)]
+        ps = [i * 16 + u for u in range(16)]
         halves = [dot_last(staged[p], pcp[p]).astype(BF16) for p in ps]
         downs = [dot(h, tra[p]) for h, p in zip(halves, ps)]
         for p, d in zip(ps, downs):
@@ -320,17 +320,14 @@
             ).astype(BF16)
             far = dot(both, bas[pl.ds(2 * p, 2)].reshape(128, 128))
             res = far + near_acc[pl.ds(2 * p, 2)].reshape(64, 128)
-            out_buf[pl.ds(2 * p, 2)] = res.astype(BF16).reshape(2, 32, 128)
-        return 0
-
-    lax.fori_loop(0, NP // 8, down, 0)
-    o = pltpu.make_async_copy(out_buf, out, out_sem)
-    o.start()
+            out[pl.ds(2 * p, 2)] = res.astype(BF16).reshape(2, 32, 128)
+        return 0
+
+    lax.fori_loop(0, NP // 16, down, 0)
     wait_part(send_buf, data_send)
     for q in range(NQ):
         wait_part(held[q].at[pl.ds(0, 15)], held_send.at[q])
     wait_part(asked.at[pl.ds(0, len(PARTNERS))], ask_send)
-    o.wait()
 
 
 def on_device(*args):
@@ -341,8 +338,8 @@
     return pl.pallas_call(
         kernel,
         out_shape=jax.ShapeDtypeStruct((NL, 32, 128), BF16),
-        in_specs=[anywhere] * 6 + [smem] * 2 + [vmem] * 2,
-        out_specs=anywhere,
+        in_specs=[anywhere]*6 + [smem] * 2 + [vmem] * 2,
+        out_specs=vmem,
         scratch_shapes=[
             pltpu.VMEM((NL + 4, 32, 128), BF16),
             pltpu.VMEM((NL, 64, 128), BF16),
@@ -370,10 +367,10 @@
             *[pltpu.VMEM((512, 4, 128), BF16)] * NQ,
         ],
         compiler_params=pltpu.CompilerParams(
-            collective_id=0, has_side_effects=True, vmem_limit_bytes=56 * 1024 * 1024
+            collective_id=0, has_side_effects=True, vmem_limit_bytes=48 * 1024 * 1024
         ),
         name="h2",
-    )(*args[:6], *[v.T for v in args[6:]])
+    )(*[pltpu.with_memory_space_constraint(a, pltpu.HBM) for a in args[:6] + tuple(v.T for v in args[6:])])
 
 
 def solution(mesh):

time: 42.3 us -> 36.5 us (0.86)
  Pallas kernels: 40.2 us -> 35.6 us
  local copies, waits for them, and re-layouts: 1.87 us -> 0.8 us
    pallas_call x1, Pallas kernels: 40.2 us -> 35.6 us  [on_device(): pl.pallas_call(kernel, out_shape=jax.ShapeDtypeStruct((NL, 32, 128), BF16...]
    unnamed x1, local copies, waits for them, and re-layouts: 1.87 us -> 0.8 us
where the time goes in v5:
time: 36.5 us; the launch traced here: 36.4 us
  Pallas kernels  35.6 us (98%)
  local copies, waits for them, and re-layouts  0.8 us (2%)
    pallas_call x1, Pallas kernels, on_device(): pl.pallas_call(kernel, out_shape=jax.ShapeDtypeStruct((NL, 32, 128), BF16...  35.6 us
    unnamed x1, local copies, waits for them, and re-layouts  0.8 us

profile of v5, /device:TPU:1, one launch (start us, length us, event | category | flops | bytes accessed | tf_op | source)
XLA Modules:
  0.0 36.4 jit_solution(16918551343193385623)
XLA Ops:
  0.0 35.6 %h2.1 = bf16[64,32,128]{2,1,0:T(8,128)(2,1)S(1)} custom-call(bf16[64,32,128]{2,1,0:T(8,128)(2,1)} %refs_0_.1, bf16[64,64,128]{2,1,0:T(8,128)(2,1)} %refs_1_.1, bf16[32,64,128]{2,1,0:T(8,128)(2,1)} %refs_2_.1, bf16[64,64,256]{2,1,0:T(8,128)(2,1)} %refs_3_.1, bf16[32,64,512]{2,1,0:T(8,128)(2,1)} %refs_4_.1, bf16[64,3,128,128]{3,2,1,0:T(8,128)(2,1)} %refs_5_.1, ...), custom_call_target="tpu_custom_call" | custom-call | tf_op jit(solution)/shard_map/h2/pallas_call | solution.py:338
  35.6 0.8 %copy.12 = bf16[64,32,128]{2,1,0:T(8,128)(2,1)} copy(bf16[64,32,128]{2,1,0:T(8,128)(2,1)S(1)} %h2.1) | data formatting | bytes 1048576

commit v6 on v5

--- a/solution.py
+++ b/solution.py
@@ -149,16 +149,18 @@
 
     pl.semaphore_wait(barrier, len(PARTNERS) + 2)
 
-    def pass_on(q, src, axis, d, sem):
+    def pass_on(q, src, half, axis, d, sem):
+        part = held[q].at[src, pl.ds(half * (NP // 2), NP // 2)]
         pltpu.make_async_remote_copy(
-            src_ref=held[q].at[src], dst_ref=held[q].at[src], send_sem=held_send.at[q],
+            src_ref=part, dst_ref=part, send_sem=held_send.at[q],
             recv_sem=sem.at[q],
             device_id=place(axis, d, 0), device_id_type=MESH,
         ).start()
 
     for q, r in enumerate(ROUTES):
         for d in (1, 3, 2):
-            pass_on(q, block[q], r[0], d, first_recv)
+            for half in range(2):
+                pass_on(q, block[q], half, r[half], d, first_recv)
     for n, p in enumerate(PARTNERS):
         back = [i for i, o in enumerate(PARTNERS) if o == (p[0], (4 - p[1]) % 4, p[2])][0]
         pltpu.make_async_remote_copy(
@@ -180,7 +182,8 @@
         halos.append(h)
     for q, r in enumerate(ROUTES):
         for d in (1, 3, 2):
-            pass_on(q, block[q], r[1], d, second_recv)
+            for half in range(2):
+                pass_on(q, block[q], half, r[1 - half], d, second_recv)
 
     before = ranks[...]
     coords = (own // 32, rem(own // 2, 4), rem(own // 16, 2) * 2 + rem(own, 2))
@@ -202,9 +205,13 @@
     for q, r in enumerate(ROUTES):
         wait_part(held[q].at[pl.ds(0, 3)], first_recv.at[q])
         for e in (1, 3, 2):
-            src = at[r[1]] * 4 + rem(at[r[0]] + e, 4)
+            src = (
+                at[r[1]] * 4 + rem(at[r[0]] + e, 4),
+                rem(at[r[1]] + e, 4) * 4 + at[r[0]],
+            )
             for d in (1, 3, 2):
-                pass_on(q, src, r[1], d, second_recv)
+                for half in range(2):
+                    pass_on(q, src[half], half, r[1 - half], d, second_recv)
 
     wait_part(asked.at[pl.ds(0, len(PARTNERS))], ask_recv)
     asked_copy = pltpu.make_async_copy(asked, asked_s, asked_sem)

time: 36.5 us -> 35.3 us (0.967); the launches traced: 36.4 us -> 34.6 us
  Pallas kernels: 35.6 us -> 33.8 us
    pallas_call x1, Pallas kernels: 35.6 us -> 33.8 us  [on_device(): pl.pallas_call(kernel, out_shape=jax.ShapeDtypeStruct((NL, 32, 128), BF16...]
where the time goes in v6:
time: 35.3 us; the launch traced here: 34.6 us
  Pallas kernels  33.8 us (96%)
  local copies, waits for them, and re-layouts  0.8 us (2%)
    pallas_call x1, Pallas kernels, on_device(): pl.pallas_call(kernel, out_shape=jax.ShapeDtypeStruct((NL, 32, 128), BF16...  33.8 us
    unnamed x1, local copies, waits for them, and re-layouts  0.8 us

profile of v6, /device:TPU:1, one launch (start us, length us, event | category | flops | bytes accessed | tf_op | source)
XLA Modules:
  0.0 34.6 jit_solution(13805626221289046906)
XLA Ops:
  0.0 33.8 %h2.1 = bf16[64,32,128]{2,1,0:T(8,128)(2,1)S(1)} custom-call(bf16[64,32,128]{2,1,0:T(8,128)(2,1)} %refs_0_.1, bf16[64,64,128]{2,1,0:T(8,128)(2,1)} %refs_1_.1, bf16[32,64,128]{2,1,0:T(8,128)(2,1)} %refs_2_.1, bf16[64,64,256]{2,1,0:T(8,128)(2,1)} %refs_3_.1, bf16[32,64,512]{2,1,0:T(8,128)(2,1)} %refs_4_.1, bf16[64,3,128,128]{3,2,1,0:T(8,128)(2,1)} %refs_5_.1, ...), custom_call_target="tpu_custom_call" | custom-call | tf_op jit(solution)/shard_map/h2/pallas_call | solution.py:345
  33.8 0.8 %copy.12 = bf16[64,32,128]{2,1,0:T(8,128)(2,1)} copy(bf16[64,32,128]{2,1,0:T(8,128)(2,1)S(1)} %h2.1) | data formatting | bytes 1048576

commit v7 on v6

--- a/solution.py
+++ b/solution.py
@@ -230,6 +230,43 @@
         pts[66:68] = jnp.zeros((2, 32, 128), BF16)
         coef[69:74] = jnp.zeros((5, 32, 128), BF16)
 
+    loads[5].wait()
+    asked_copy.wait()
+    slot_copy.wait()
+
+    base = core * 8
+    for q, r in enumerate(ROUTES):
+        wait_part(held[q].at[pl.ds(0, 12)], second_recv.at[q])
+        fixed = adds[r[2]](at[r[2]])
+        fixed = base + fixed[0] * 8 + fixed[1]
+
+        def gather(ref, offset, n):
+            def some(i, _):
+                add2 = adds[r[1]](i)
+                for j in range(4):
+                    add1 = adds[r[0]](jnp.int32(j))
+                    who = fixed + (add1[0] + add2[0]) * 8 + add1[1] + add2[1]
+                    for c in range(CAP):
+                        ref[offset + (i * 4 + j) * CAP + c] = held[q][
+                            i * 4 + j, asked_s[n, c, who]
+                        ]
+                return 0
+
+            lax.fori_loop(0, 4, some, 0)
+
+        mine = (at[r[2]] * 2 + core) * 64
+        line = [(i, p) for i, p in enumerate(PARTNERS) if p[0] == r[2] and p[1]]
+        line.append((len(PARTNERS) - 1, PARTNERS[-1]))
+        for m, (n, p) in enumerate(line):
+            start = (q * 7 + m) * 64
+            gather(send_buf, start, n)
+            pltpu.make_async_remote_copy(
+                src_ref=send_buf.at[pl.ds(start, 64)], dst_ref=recv_buf[q].at[pl.ds(mine, 64)],
+                send_sem=data_send, recv_sem=data_recv.at[q],
+                device_id=place(r[2], p[1], p[2]), device_id_type=MESH,
+            ).start()
+        gather(recv_buf[q], mine, len(PARTNERS))
+
     loads[4].wait()
 
     def leaf_body(i, _):
@@ -248,43 +285,6 @@
         return 0
 
     lax.fori_loop(0, NP // 8, leaf_body, 0)
-    loads[5].wait()
-    asked_copy.wait()
-    slot_copy.wait()
-
-    base = core * 8
-    for q, r in enumerate(ROUTES):
-        wait_part(held[q].at[pl.ds(0, 12)], second_recv.at[q])
-        fixed = adds[r[2]](at[r[2]])
-        fixed = base + fixed[0] * 8 + fixed[1]
-
-        def gather(ref, offset, n):
-            def some(i, _):
-                add2 = adds[r[1]](i)
-                for j in range(4):
-                    add1 = adds[r[0]](jnp.int32(j))
-                    who = fixed + (add1[0] + add2[0]) * 8 + add1[1] + add2[1]
-                    for c in range(CAP):
-                        ref[offset + (i * 4 + j) * CAP + c] = held[q][
-                            i * 4 + j, asked_s[n, c, who]
-                        ]
-                return 0
-
-            lax.fori_loop(0, 4, some, 0)
-
-        mine = (at[r[2]] * 2 + core) * 64
-        line = [(i, p) for i, p in enumerate(PARTNERS) if p[0] == r[2] and p[1]]
-        line.append((len(PARTNERS) - 1, PARTNERS[-1]))
-        for m, (n, p) in enumerate(line):
-            start = (q * 7 + m) * 64
-            gather(send_buf, start, n)
-            pltpu.make_async_remote_copy(
-                src_ref=send_buf.at[pl.ds(start, 64)], dst_ref=recv_buf[q].at[pl.ds(mine, 64)],
-                send_sem=data_send, recv_sem=data_recv.at[q],
-                device_id=place(r[2], p[1], p[2]), device_id_type=MESH,
-            ).start()
-        gather(recv_buf[q], mine, len(PARTNERS))
-
     loads[3].wait()
 
     def near_body(i, _):
@@ -313,9 +313,12 @@
                     staged[p, 8 * q + 4:8 * q + 8, cols] = jnp.where(low4, pltpu.roll(va, 64, 1), vb)
             return 0
 
-        lax.fori_loop(0, NP // 8, stage, 0)
+        if q < NQ - 1:
+            lax.fori_loop(0, NP // 8, stage, 0)
 
     def down(i, _):
+        for h in range(2):
+            stage(i * 2 + h, 0)
         ps = [i * 16 + u for u in range(16)]
         halves = [dot_last(staged[p], pcp[p]).astype(BF16) for p in ps]
         downs = [dot(h, tra[p]) for h, p in zip(halves, ps)]

time: 35.3 us -> 34.4 us (0.975); the launches traced: 34.6 us -> 34.2 us
  Pallas kernels: 33.8 us -> 33.4 us
    pallas_call x1, Pallas kernels: 33.8 us -> 33.4 us  [on_device(): pl.pallas_call(kernel, out_shape=jax.ShapeDtypeStruct((NL, 32, 128), BF16...]
where the time goes in v7:
time: 34.4 us; the launch traced here: 34.2 us
  Pallas kernels  33.4 us (97%)
  local copies, waits for them, and re-layouts  0.8 us (2%)
    pallas_call x1, Pallas kernels, on_device(): pl.pallas_call(kernel, out_shape=jax.ShapeDtypeStruct((NL, 32, 128), BF16...  33.4 us
    unnamed x1, local copies, waits for them, and re-layouts  0.8 us

profile of v7, /device:TPU:1, one launch (start us, length us, event | category | flops | bytes accessed | tf_op | source)
XLA Modules:
  0.0 34.2 jit_solution(15520183712200693515)
XLA Ops:
  0.0 33.4 %h2.1 = bf16[64,32,128]{2,1,0:T(8,128)(2,1)S(1)} custom-call(bf16[64,32,128]{2,1,0:T(8,128)(2,1)} %refs_0_.1, bf16[64,64,128]{2,1,0:T(8,128)(2,1)} %refs_1_.1, bf16[32,64,128]{2,1,0:T(8,128)(2,1)} %refs_2_.1, bf16[64,64,256]{2,1,0:T(8,128)(2,1)} %refs_3_.1, bf16[32,64,512]{2,1,0:T(8,128)(2,1)} %refs_4_.1, bf16[64,3,128,128]{3,2,1,0:T(8,128)(2,1)} %refs_5_.1, ...), custom_call_target="tpu_custom_call" | custom-call | tf_op jit(solution)/shard_map/h2/pallas_call | solution.py:348
  33.4 0.8 %copy.12 = bf16[64,32,128]{2,1,0:T(8,128)(2,1)} copy(bf16[64,32,128]{2,1,0:T(8,128)(2,1)S(1)} %h2.1) | data formatting | bytes 1048576
